TPU v7x, 32 devices: a whole 2x2x4 slice. The times are simulated.
32 devices in a mesh: pipe: 4 (over z), dp: 4 (over y, x), tensor: 2 (over core).
Axes of the slice: x: 2, y: 2, z: 4, core: 2. Of those that a mesh axis runs over, the one named last changes fastest.
Arguments:
- saved_inputs: bfloat16 [3, 2, 4, 512, 4096], P(None, None, 'pipe', 'dp', 'tensor'), may hold values from -6 to 6
- proj_in: bfloat16 [2, 4, 512, 4096], P(None, 'pipe', None, 'tensor'), may hold values from -0.09375 to 0.09375
- proj_out: bfloat16 [2, 4, 512, 4096], P(None, 'pipe', None, 'tensor'), may hold values from -0.25 to 0.25
- norm_gain: float32 [2, 4, 4096], P(None, 'pipe', 'tensor'), may hold values from 0.1 to 1.9
- arriving: bfloat16 [2, 4, 512, 4096], P(None, 'pipe', 'dp', 'tensor'), may hold values from -6 to 6
- logp_grad: bfloat16 [2, 512, 4096], P(None, 'dp', 'tensor'), may hold values from -6 to 6
- rewards: float32 [2, 4, 4], P(None, 'dp'), may hold values from -4 to 4
- seq_lengths: int32 [2, 4, 4], P(None, 'dp'), may hold values from 1 to 64, 128 in all within a row
- group_ids: int32 [2, 4, 4], P(None, 'dp'), may hold values from 0 to 3
Outputs:
- grad_in: float32 [2, 4, 512, 4096], P(None, 'pipe', 'dp', 'tensor')
- grad_out: float32 [2, 4, 512, 4096], P(None, 'pipe', 'dp', 'tensor')
- leaving: bfloat16 [2, 4, 512, 4096], P(None, 'pipe', 'dp', 'tensor')
Inputs may be any that keep to these rules, and one draw needn't show every extreme that they name: `seq_lengths`: the 4 lengths of one microbatch on one replica sum to 128. `group_ids`: groups take sequences from several replicas and microbatches.
All inputs are finite; a program needn't handle non-finite values.
Results may differ from a plain program's by a relative error of at most 0.023.
Values may be sent and summed in bfloat16 or wider, within the bound.
A program may use at most 128 MiB of HBM per device.

v0:
```python
import jax
import jax.numpy as jnp
from jax import lax
from jax.sharding import PartitionSpec as P

D = 4096
EPS = 1e-05


def shifted(x, axis, by):
    count = lax.axis_size(axis)
    return lax.ppermute(x, axis, [(i, (i + by) % count) for i in range(count)])


def silu_slope(values):
    sigma = jax.nn.sigmoid(values)
    return sigma * (1.0 + values * (1.0 - sigma))


def block_back(inputs, arrive, weight_in, weight_out, gain_rows, inv_rms):
    inputs_f = inputs.astype(jnp.float32)
    gained = (inputs_f * gain_rows[:, None, :]).astype(jnp.bfloat16)
    part_pre = jnp.einsum("vrd,vkd->vrk", gained, weight_in, preferred_element_type=jnp.float32)
    part_back = jnp.einsum("vrd,vkd->vrk", arrive, weight_out, preferred_element_type=jnp.float32)
    pre_sum, back_sum = (
        lax.psum(part_pre.astype(jnp.bfloat16), "tensor").astype(jnp.float32),
        lax.psum(part_back.astype(jnp.bfloat16), "tensor").astype(jnp.float32),
    )
    scaled = inv_rms[..., None]
    pre_act = scaled * pre_sum
    hidden = jax.nn.silu(pre_act).astype(jnp.bfloat16)
    grad_pre = back_sum * silu_slope(pre_act)
    grad_scaled = (scaled * grad_pre).astype(jnp.bfloat16)
    term_in = jnp.einsum("vrk,vrd->vkd", grad_scaled, gained, preferred_element_type=jnp.float32)
    term_out = jnp.einsum("vrk,vrd->vkd", hidden, arrive, preferred_element_type=jnp.float32)
    grad_gained = jnp.einsum(
        "vrk,vkd->vrd", grad_scaled, weight_in, preferred_element_type=jnp.float32
    )
    radial_sum = jnp.sum(grad_pre * pre_sum, axis=-1)
    out_cot = (
        arrive.astype(jnp.float32)
        + gain_rows[:, None, :] * grad_gained
        - inputs_f * (inv_rms**3 * radial_sum / D)[..., None]
    )
    return (out_cot.astype(jnp.bfloat16), term_in, term_out)


def shards(
    saved_inputs, proj_in, proj_out, norm_gain, arriving, logp_grad, rewards, seq_lengths, group_ids
):
    sections = lax.axis_size("pipe")
    section = lax.axis_index("pipe")
    replicas = lax.axis_size("dp")
    saved = saved_inputs[:, :, 0]
    weights_in = proj_in[:, 0]
    weights_out = proj_out[:, 0]
    gains = norm_gain[:, 0]
    current = arriving[:, 0]
    step_count = saved.shape[0]
    local_rows = saved.shape[2]
    new_count = logp_grad.shape[0]
    seq_count = rewards.shape[2]
    group_count = new_count * replicas * seq_count // 8
    saved_f = saved.astype(jnp.float32)
    squares = jnp.sum(saved_f * saved_f, axis=-1)
    totals = lax.psum(squares, "tensor")
    inv_rms_all = 1.0 / jnp.sqrt(totals / D + EPS)
    groups = jnp.arange(group_count, dtype=jnp.int32)
    member = (group_ids[..., None] == groups).astype(jnp.float32)
    sums = jnp.sum(member * rewards[..., None], axis=(0, 1, 2))
    counts = jnp.sum(member, axis=(0, 1, 2))
    sums, counts = lax.psum((sums, counts), "dp")
    means = sums / jnp.maximum(counts, 1.0)
    advantage = rewards - jnp.sum(member * means, axis=-1)
    ends = jnp.cumsum(seq_lengths, axis=-1)
    position = jnp.arange(local_rows, dtype=jnp.int32)
    segment = jnp.sum((position[:, None] >= ends[..., None, :]).astype(jnp.int32), axis=-1)
    pick = (segment[..., None] == jnp.arange(seq_count, dtype=jnp.int32)).astype(jnp.float32)
    token_weight = jnp.sum(pick * advantage[..., None, :], axis=-1)[:, 0]
    entering = (-token_weight[..., None] * logp_grad.astype(jnp.float32)).astype(jnp.bfloat16)

    def run_blocks(first, last, arrive, step_index):
        return block_back(
            saved[step_index, first:last],
            arrive,
            weights_in,
            weights_out,
            gains,
            inv_rms_all[step_index, first:last],
        )

    is_top = section == sections - 1
    acc_in = jnp.zeros((2,) + weights_in.shape[1:], jnp.float32)
    acc_out = jnp.zeros((2,) + weights_in.shape[1:], jnp.float32)
    for step_index in range(step_count - 1):
        moved, add_in, add_out = run_blocks(0, 2, current, step_index)
        acc_in = acc_in + add_in
        acc_out = acc_out + add_out
        received = shifted(moved, "pipe", -1)
        from_upper = received[1]
        from_lower = received[0]
        upper_next = jnp.where(is_top, entering[step_index], from_upper)
        lower_next = jnp.where(is_top, from_upper, from_lower)
        current = jnp.stack([lower_next, upper_next])
    final_index = step_count - 1
    leaving, add_in, add_out = run_blocks(0, 2, current, final_index)
    summed_in, summed_out = (
        lax.psum_scatter(
            (acc_in + add_in).astype(jnp.bfloat16), "dp", scatter_dimension=1, tiled=True
        ).astype(jnp.float32),
        lax.psum_scatter(
            (acc_out + add_out).astype(jnp.bfloat16), "dp", scatter_dimension=1, tiled=True
        ).astype(jnp.float32),
    )
    scale = 1.0 / (replicas * local_rows)
    return ((summed_in * scale)[:, None], (summed_out * scale)[:, None], leaving[:, None])


def solution(mesh):
    return jax.shard_map(
        shards,
        mesh=mesh,
        in_specs=(
            P(None, None, "pipe", "dp", "tensor"),
            P(None, "pipe", None, "tensor"),
            P(None, "pipe", None, "tensor"),
            P(None, "pipe", "tensor"),
            P(None, "pipe", "dp", "tensor"),
            P(None, "dp", "tensor"),
            P(None, "dp", None),
            P(None, "dp", None),
            P(None, "dp", None),
        ),
        out_specs=(
            P(None, "pipe", "dp", "tensor"),
            P(None, "pipe", "dp", "tensor"),
            P(None, "pipe", "dp", "tensor"),
        ),
        check_vma=False,
    )
```

profile of v0, /device:TPU:0, one launch (start us, length us, event | category | flops | bytes accessed | tf_op | source)
XLA Modules:
  0.0 281.6 jit_solution(14688957267595545626)
XLA Ops:
  8.1 4.8 %fusion.43 = bf16[2,128,512]{2,1,0:T(8,128)(2,1)} fusion(bf16[2,1,512,2048]{3,2,1,0:T(8,128)(2,1)} %param.11, bf16[2,1,128,2048]{3,2,1,0:T(8,128)(2,1)} %param.13), kind=kOutput, calls=%fused_computation.43 | convolution fusion | flops 537001984 | bytes 5505024 | tf_op jit(solution)/shard_map/vrd,vkd->vrk/dot_general | solution.py:24
  12.9 4.4 %fusion.52 = bf16[2,128,512]{2,1,0:T(8,128)(2,1)} fusion(bf16[2,1,512,2048]{3,2,1,0:T(8,128)(2,1)} %param.10, f32[2,2048]{1,0:T(2,128)S(1)} %bitcast.130, bf16[3,2,1,128,2048]{4,3,1,2,0:T(8,128)(2,1)S(1)} %bitcast.121), kind=kOutput, calls=%fused_computation.46 | convolution fusion | flops 538574848 | bytes 5521408 | tf_op jit(solution)/shard_map/vrd,vkd->vrk/dot_general | solution.py:23
  18.2 11.4 %all-reduce = (f32[4]{0:T(128)S(1)}, f32[4]{0:T(128)S(1)}) all-reduce(f32[4]{0:T(128)S(1)} %get-tuple-element.10, f32[4]{0:T(128)S(1)} %get-tuple-element.9), channel_id=1, replica_groups=mesh['pipe'=4,'dp'=4,'tensor'=2] {'dp'}, use_global_device_ids=true, to_apply=%region_8.9 | all-reduce | flops 8 | bytes 64 | tf_op jit(solution)/shard_map/psum | solution.py:72
  29.9 2.4 psum.63
  32.4 6.5 %all-reduce.12.cloned.1.call-done = (bf16[2,128,512]{2,1,0:T(8,128)(2,1)}, bf16[2,128,512]{2,1,0:T(8,128)(2,1)}) async-done(((bf16[2,128,512]{2,1,0:T(8,128)(2,1)}, bf16[2,128,512]{2,1,0:T(8,128)(2,1)}), (bf16[2,128,512]{2,1,0:T(8,128)(2,1)}, bf16[2,128,512]{2,1,0:T(8,128)(2,1)})) %all-reduce.12.cloned.1.call-update) | async-done | bytes 524304 | tf_op jit(solution)/shard_map/psum | solution.py:26
  38.9 1.4 fusion.93
  40.3 5.0 %fusion.33 = bf16[2,128,2048]{2,1,0:T(8,128)(2,1)} fusion(bf16[2,1,512,2048]{3,2,1,0:T(8,128)(2,1)} %param.10, bf16[2,1,128,2048]{3,2,1,0:T(8,128)(2,1)} %param.13, f32[2,128]{1,0:T(2,128)S(1)} %fusion.121, f32[2,2048]{1,0:T(2,128)S(1)} %bitcast.131, bf16[3,2,1,128,2048]{4,3,1,2,0:T(8,128)(2,1)S(1)} %bitcast.122, f32[2,128]{1,0:T(2,128)S(1)} %get-tuple-element.25, ...), kind=kOutput, calls=%fused_computation.32 | convolution fusion | flops 542244864 | bytes 7882752 | tf_op jit(solution)/shard_map/vrk,vkd->vrd/dot_general | solution.py:36
  45.3 3.6 %collective-permute-start = (bf16[2,128,2048]{2,1,0:T(8,128)(2,1)}, bf16[2,128,2048]{2,1,0:T(8,128)(2,1)}, u32[]{:S(2)}, u32[]{:S(2)}) collective-permute-start(bf16[2,128,2048]{2,1,0:T(8,128)(2,1)} %fusion.33), channel_id=1, source_target_pairs={{0,24},{8,0},{16,8},{24,16},{1,25},{9,1},{17,9},{25,17},{2,26},{10... | collective-permute-start | bytes 3145736 | tf_op jit(solution)/shard_map/ppermute | solution.py:12
  49.1 4.5 %fusion.55 = bf16[2,128,512]{2,1,0:T(8,128)(2,1)} fusion(bf16[2,1,512,2048]{3,2,1,0:T(8,128)(2,1)} %param.10, f32[2,2048]{1,0:T(2,128)S(1)} %bitcast.132, bf16[3,2,1,128,2048]{4,3,1,2,0:T(8,128)(2,1)S(1)} %bitcast.123), kind=kOutput, calls=%fused_computation.47 | convolution fusion | flops 538574848 | bytes 5521408 | tf_op jit(solution)/shard_map/vrd,vkd->vrk/dot_general | solution.py:23
  53.9 18.2 %collective-permute-done = bf16[2,128,2048]{2,1,0:T(8,128)(2,1)} collective-permute-done((bf16[2,128,2048]{2,1,0:T(8,128)(2,1)}, bf16[2,128,2048]{2,1,0:T(8,128)(2,1)}, u32[]{:S(2)}, u32[]{:S(2)}) %collective-permute-start) | collective-permute-done | bytes 1048608 | tf_op jit(solution)/shard_map/ppermute | solution.py:12
  72.1 1.3 slice_select_fusion.3
  74.3 2.2 fusion.46
  76.6 20.6 %all-reduce.10.cloned.1.call-done = (bf16[2,128,512]{2,1,0:T(8,128)(2,1)}, bf16[2,128,512]{2,1,0:T(8,128)(2,1)}) async-done(((bf16[2,128,512]{2,1,0:T(8,128)(2,1)}, bf16[2,128,512]{2,1,0:T(8,128)(2,1)}), (bf16[2,128,512]{2,1,0:T(8,128)(2,1)}, bf16[2,128,512]{2,1,0:T(8,128)(2,1)})) %all-reduce.10.cloned.1.call-update) | async-done | bytes 524304 | tf_op jit(solution)/shard_map/psum | solution.py:26
  97.2 1.4 fusion.101
  98.7 4.1 %fusion.39 = bf16[2,128,2048]{2,1,0:T(8,128)(2,1)S(1)} fusion(f32[2,128]{1,0:T(2,128)S(1)} %fusion.123, bf16[2,1,512,2048]{3,2,1,0:T(8,128)(2,1)} %param.10, f32[2,2048]{1,0:T(2,128)S(1)} %bitcast.133, bf16[3,2,1,128,2048]{4,3,1,2,0:T(8,128)(2,1)S(1)} %bitcast.124, bf16[1,128,2048]{2,1,0:T(8,128)(2,1)} %copy-done.13, bf16[1,128,2048]{2,1,0:T(8,128)(2,1)} %copy-done.11, ...), kind=kOutput, calls=%fused_computation.36 | convolution fusion | flops 542769152 | bytes 7882752 | tf_op jit(solution)/shard_map/vrk,vkd->vrd/dot_general | solution.py:36
  102.8 3.7 %collective-permute-start.1 = (bf16[2,128,2048]{2,1,0:T(8,128)(2,1)S(1)}, bf16[2,128,2048]{2,1,0:T(8,128)(2,1)S(1)}, u32[]{:S(2)}, u32[]{:S(2)}) collective-permute-start(bf16[2,128,2048]{2,1,0:T(8,128)(2,1)S(1)} %fusion.39), channel_id=1, source_target_pairs={{0,24},{8,0},{16,8},{24,16},{1,25},{9,1},{17,9},{25,17},{2,26},{10... | collective-permute-start | bytes 3145736 | tf_op jit(solution)/shard_map/ppermute | solution.py:12
  106.5 2.2 fusion.58
  108.7 20.6 %collective-permute-done.1 = bf16[2,128,2048]{2,1,0:T(8,128)(2,1)S(1)} collective-permute-done((bf16[2,128,2048]{2,1,0:T(8,128)(2,1)S(1)}, bf16[2,128,2048]{2,1,0:T(8,128)(2,1)S(1)}, u32[]{:S(2)}, u32[]{:S(2)}) %collective-permute-start.1) | collective-permute-done | bytes 1048608 | tf_op jit(solution)/shard_map/ppermute | solution.py:12
  130.4 2.2 fusion.49
  132.9 5.9 %fusion.62 = f32[2,512,2048]{2,1,0:T(8,128)} fusion(bf16[2,1,128,2048]{3,2,1,0:T(8,128)(2,1)} %param.13, bf16[2,128,512]{2,1,0:T(8,128)(2,1)S(1)} %copy-done.6, f32[2,128]{1,0:T(2,128)S(1)} %get-tuple-element.25), kind=kOutput, calls=%fused_computation.55 | convolution fusion | flops 537788416 | bytes 9700352 | tf_op jit(solution)/shard_map/vrk,vrd->vkd/dot_general | solution.py:35
  138.9 4.6 %fusion.110 = f32[2,512,2048]{2,1,0:T(8,128)} fusion(bf16[1,128,2048]{2,1,0:T(8,128)(2,1)S(1)} %copy-done.14, bf16[1,128,2048]{2,1,0:T(8,128)(2,1)S(1)} %copy-done.12, bf16[2,128,512]{2,1,0:T(8,128)(2,1)S(1)} %copy-done.7, f32[2,128]{1,0:T(2,128)S(1)} %get-tuple-element.24), kind=kOutput, calls=%fused_computation.106 | convolution fusion | flops 538312704 | bytes 9700352 | tf_op jit(solution)/shard_map/vrk,vrd->vkd/dot_general | solution.py:35
  143.4 9.9 %all-reduce.8.cloned.1.call-done = (bf16[2,128,512]{2,1,0:T(8,128)(2,1)}, bf16[2,128,512]{2,1,0:T(8,128)(2,1)}) async-done(((bf16[2,128,512]{2,1,0:T(8,128)(2,1)}, bf16[2,128,512]{2,1,0:T(8,128)(2,1)}), (bf16[2,128,512]{2,1,0:T(8,128)(2,1)}, bf16[2,128,512]{2,1,0:T(8,128)(2,1)})) %all-reduce.8.cloned.1.call-update) | async-done | bytes 524304 | tf_op jit(solution)/shard_map/psum | solution.py:26
  153.3 9.5 %add_convert_fusion = bf16[2,512,2048]{2,1,0:T(8,128)(2,1)} fusion(f32[2,512,2048]{2,1,0:T(8,128)} %fusion.62, f32[2,512,2048]{2,1,0:T(8,128)} %fusion.110, bf16[1,128,2048]{2,1,0:T(8,128)(2,1)} %copy-done.10, bf16[1,128,2048]{2,1,0:T(8,128)(2,1)} %copy-done.9, bf16[2,128,512]{2,1,0:T(8,128)(2,1)} %get-tuple-element.13, f32[2,128]{1,0:T(2,128)S(1)} %get-tuple-element.23), kind=kOutput, calls=%fused_computation | convolution fusion | flops 544604160 | bytes 22283264 | tf_op jit(solution)/shard_map/vrk,vrd->vkd/dot_general | solution.py:35
  162.9 2.4 fusion.74
  165.4 1.4 fusion.71
  166.9 3.7 %add_convert_fusion.1 = bf16[2,512,2048]{2,1,0:T(8,128)(2,1)} fusion(f32[2,512,2048]{2,1,0:T(8,128)S(1)} %fusion.74, f32[2,512,2048]{2,1,0:T(8,128)S(1)} %fusion.71, f32[2,2048]{1,0:T(2,128)S(1)} %bitcast.137, bf16[3,2,1,128,2048]{4,3,1,2,0:T(8,128)(2,1)S(1)} %bitcast.128, f32[2,128]{1,0:T(2,128)S(1)} %get-tuple-element.23, ...), kind=kOutput, calls=%fused_computation.1 | convolution fusion | flops 546439168 | bytes 22561792 | tf_op jit(solution)/shard_map/vrk,vrd->vkd/dot_general | solution.py:34
  170.5 1.4 fusion.109
  172.0 4.8 %fusion.61 = bf16[2,1,128,2048]{3,2,1,0:T(8,128)(2,1)} fusion(f32[2,128]{1,0:T(2,128)S(1)} %fusion.125, bf16[2,1,512,2048]{3,2,1,0:T(8,128)(2,1)} %param.10, f32[2,2048]{1,0:T(2,128)S(1)} %bitcast.138, bf16[3,2,1,128,2048]{4,3,1,2,0:T(8,128)(2,1)S(1)} %bitcast.129, bf16[1,128,2048]{2,1,0:T(8,128)(2,1)} %copy-done.10, bf16[1,128,2048]{2,1,0:T(8,128)(2,1)} %copy-done.9, ...), kind=kOutput, calls=%fused_computation.49 | convolution fusion | flops 542769152 | bytes 7882752 | tf_op jit(solution)/shard_map/vrk,vkd->vrd/dot_general | solution.py:36
  176.9 40.0 %reduce-scatter.5.cloned.1.call-done = bf16[2,128,2048]{2,1,0:T(8,128)(2,1)} async-done(((bf16[2,512,2048]{2,1,0:T(8,128)(2,1)}), bf16[2,128,2048]{2,1,0:T(8,128)(2,1)}) %reduce-scatter.5.cloned.1.call-update) | async-done | bytes 1048592 | tf_op jit(solution)/shard_map/reduce_scatter | solution.py:111
  216.8 2.8 multiply_bitcast_fusion
  219.6 52.7 %reduce-scatter.3.cloned.1.call-done = bf16[2,128,2048]{2,1,0:T(8,128)(2,1)} async-done(((bf16[2,512,2048]{2,1,0:T(8,128)(2,1)}), bf16[2,128,2048]{2,1,0:T(8,128)(2,1)}) %reduce-scatter.3.cloned.1.call-update) | async-done | bytes 1048592 | tf_op jit(solution)/shard_map/reduce_scatter | solution.py:108
  272.3 2.8 multiply_bitcast_fusion.1
  (71 shorter events, 5.0 us)
Async XLA Ops:
  7.2 5.7 %copy-start = (bf16[3,2,1,128,2048]{4,3,2,1,0:T(8,128)(2,1)S(1)}, bf16[3,2,1,128,2048]{4,3,2,1,0:T(8,128)(2,1)}, u32[]{:S(2)}) copy-start(bf16[3,2,1,128,2048]{4,3,2,1,0:T(8,128)(2,1)} %param.9) | copy-start | bytes 9437188
  7.2 31.7 %all-reduce.12.cloned.1.call-start = ((), (), s32[]{:S(2)}) async-start(), calls=%async_computation.6 | async-start | bytes 1048576 | tf_op jit(solution)/shard_map/psum | solution.py:26
  17.3 0.8 copy-start.18
  17.3 0.8 copy-start.19
  17.3 12.4 %copy-start.20 = (s32[2,1,4]{2,1,0:T(1,128)S(1)}, s32[2,1,4]{2,1,0:T(1,128)}, u32[]{:S(2)}) copy-start(s32[2,1,4]{2,1,0:T(1,128)} %param.16) | copy-start | bytes 100
  17.3 79.9 %all-reduce.10.cloned.1.call-start = ((), (), s32[]{:S(2)}) async-start(), calls=%async_computation.5 | async-start | bytes 1048576 | tf_op jit(solution)/shard_map/psum | solution.py:26
  45.3 26.8 %collective-permute-start = (bf16[2,128,2048]{2,1,0:T(8,128)(2,1)}, bf16[2,128,2048]{2,1,0:T(8,128)(2,1)}, u32[]{:S(2)}, u32[]{:S(2)}) collective-permute-start(bf16[2,128,2048]{2,1,0:T(8,128)(2,1)} %fusion.33), channel_id=1, source_target_pairs={{0,24},{8,0},{16,8},{24,16},{1,25},{9,1},{17,9},{25,17},{2,26},{10... | collective-permute-start | bytes 3145736 | tf_op jit(solution)/shard_map/ppermute | solution.py:12
  49.1 4.5 %copy-start.17 = (bf16[2,128,2048]{2,1,0:T(8,128)(2,1)S(1)}, bf16[2,128,2048]{2,1,0:T(8,128)(2,1)}, u32[]{:S(2)}) copy-start(bf16[2,128,2048]{2,1,0:T(8,128)(2,1)} %param.14) | copy-start | bytes 3145732
  53.6 20.7 %copy-start.1 = (bf16[2,1,512,2048]{3,2,1,0:T(8,128)(2,1)S(1)}, bf16[2,1,512,2048]{3,2,1,0:T(8,128)(2,1)}, u32[]{:S(2)}) copy-start(bf16[2,1,512,2048]{3,2,1,0:T(8,128)(2,1)} %param.11) | copy-start | bytes 12582916
  53.9 18.2 %copy-start.3 = (bf16[2,128,2048]{2,1,0:T(8,128)(2,1)}, bf16[2,128,2048]{2,1,0:T(8,128)(2,1)S(1)}, u32[]{:S(2)}) copy-start(bf16[2,128,2048]{2,1,0:T(8,128)(2,1)S(1)} %multiply_convert_fusion) | copy-start | bytes 3145732
  73.4 0.8 copy-start.11
  73.4 1.0 copy-start.13
  76.6 76.8 %all-reduce.8.cloned.1.call-start = ((), (), s32[]{:S(2)}) async-start(), calls=%async_computation.4 | async-start | bytes 1048576 | tf_op jit(solution)/shard_map/psum | solution.py:26
  98.7 7.8 %copy-start.21 = (bf16[2,1,512,2048]{3,2,1,0:T(8,128)(2,1)S(1)}, bf16[2,1,512,2048]{3,2,1,0:T(8,128)(2,1)}, u32[]{:S(2)}) copy-start(bf16[2,1,512,2048]{3,2,1,0:T(8,128)(2,1)} %param.10) | copy-start | bytes 12582916
  102.8 26.6 %copy-start.4 = (bf16[2,128,2048]{2,1,0:T(8,128)(2,1)S(1)}, bf16[2,128,2048]{2,1,0:T(8,128)(2,1)}, u32[]{:S(2)}) copy-start(bf16[2,128,2048]{2,1,0:T(8,128)(2,1)} %copy-done.3) | copy-start | bytes 3145732
  102.8 27.6 %copy-start.2 = (bf16[2,1,512,2048]{3,2,1,0:T(8,128)(2,1)S(1)}, bf16[2,1,512,2048]{3,2,1,0:T(8,128)(2,1)}, u32[]{:S(2)}) copy-start(bf16[2,1,512,2048]{3,2,1,0:T(8,128)(2,1)} %param.11) | copy-start | bytes 12582916
  102.8 26.5 %collective-permute-start.1 = (bf16[2,128,2048]{2,1,0:T(8,128)(2,1)S(1)}, bf16[2,128,2048]{2,1,0:T(8,128)(2,1)S(1)}, u32[]{:S(2)}, u32[]{:S(2)}) collective-permute-start(bf16[2,128,2048]{2,1,0:T(8,128)(2,1)S(1)} %fusion.39), channel_id=1, source_target_pairs={{0,24},{8,0},{16,8},{24,16},{1,25},{9,1},{17,9},{25,17},{2,26},{10... | collective-permute-start | bytes 3145736 | tf_op jit(solution)/shard_map/ppermute | solution.py:12
  129.4 0.8 copy-start.9
  129.5 1.0 copy-start.10
  129.5 3.4 %copy-start.6 = (bf16[2,128,512]{2,1,0:T(8,128)(2,1)S(1)}, bf16[2,128,512]{2,1,0:T(8,128)(2,1)}, u32[]{:S(2)}) copy-start(bf16[2,128,512]{2,1,0:T(8,128)(2,1)} %get-tuple-element.17) | copy-start | bytes 786436
  132.6 84.2 %reduce-scatter.5.cloned.1.call-start = ((), (), s32[]{:S(2)}) async-start(), calls=%async_computation.3 | async-start | bytes 5242880 | tf_op jit(solution)/shard_map/reduce_scatter | solution.py:111
  132.9 6.0 %copy-start.7 = (bf16[2,128,512]{2,1,0:T(8,128)(2,1)S(1)}, bf16[2,128,512]{2,1,0:T(8,128)(2,1)}, u32[]{:S(2)}) copy-start(bf16[2,128,512]{2,1,0:T(8,128)(2,1)} %get-tuple-element.15) | copy-start | bytes 786436
  132.9 6.0 %copy-start.12 = (bf16[1,128,2048]{2,1,0:T(8,128)(2,1)S(1)}, bf16[1,128,2048]{2,1,0:T(8,128)(2,1)}, u32[]{:S(2)}) copy-start(bf16[1,128,2048]{2,1,0:T(8,128)(2,1)} %copy-done.11) | copy-start | bytes 1572868
  132.9 5.9 %copy-start.14 = (bf16[1,128,2048]{2,1,0:T(8,128)(2,1)S(1)}, bf16[1,128,2048]{2,1,0:T(8,128)(2,1)}, u32[]{:S(2)}) copy-start(bf16[1,128,2048]{2,1,0:T(8,128)(2,1)} %copy-done.13) | copy-start | bytes 1572868
  162.9 109.4 %reduce-scatter.3.cloned.1.call-start = ((), (), s32[]{:S(2)}) async-start(), calls=%async_computation.2 | async-start | bytes 5242880 | tf_op jit(solution)/shard_map/reduce_scatter | solution.py:108
  162.9 2.5 copy-start.8
  162.9 2.5 copy-start.16
  165.4 1.5 copy-start.5
  165.4 1.5 copy-start.15
Sparse Core Ops, SparseCore 0:
  17.4 21.3 all-reduce.11
  76.7 20.5 all-reduce.9
  132.8 20.5 all-reduce.7
  163.0 53.7 reduce-scatter.4
  219.6 52.6 reduce-scatter.2
where the time goes:
time: 282 us
  waiting for transfers between devices  169 us (60%)
  matrix products  61.7 us (22%)
  between operations  14.1 us (5%)
  blocking collectives  13.8 us (5%)
  other arithmetic  12.9 us (5%)
  starting transfers between devices  7.7 us (3%)
  local copies, waits for them, and re-layouts  2.86 us (1%)
    reduce_scatter x1, waiting for transfers between devices, shards(): lax.psum_scatter((acc_in + add_in).astype(jnp.bfloat16), 'dp', scatter_di...  52.7 us
    reduce_scatter x1, waiting for transfers between devices, shards(): lax.psum_scatter((acc_out + add_out).astype(jnp.bfloat16), 'dp', scatter_...  40 us
    ppermute x2, waiting for transfers between devices, shifted(): return lax.ppermute(x, axis, [(i, (i + by) % count) for i in range(count)])  38.8 us
    psum x3, waiting for transfers between devices, block_back(): lax.psum(part_pre.astype(jnp.bfloat16), 'tensor').astype(jnp.float32)  37 us
    dot_general x3, matrix products, block_back(): jnp.einsum('vrk,vrd->vkd', hidden, arrive, preferred_element_type=jnp.flo...  20 us
    dot_general x3, matrix products, block_back(): jnp.einsum('vrk,vkd->vrd', grad_scaled, weight_in, preferred_element_type...  13.9 us
    psum x1, blocking collectives, shards(): sums, counts = lax.psum((sums, counts), 'dp')  11.4 us
    dot_general x3, matrix products, block_back(): jnp.einsum('vrd,vkd->vrk', gained, weight_in, preferred_element_type=jnp....  11.1 us
  transfers between devices with their start and end apart: 7, of which 7 were waited for; matrix products, arithmetic and copies ran while one was open for 13% of the time, Pallas kernels for 0%

commit v1 on v0

--- a/solution.py
+++ b/solution.py
@@ -23,7 +23,9 @@
     part_pre = jnp.einsum("vrd,vkd->vrk", gained, weight_in, preferred_element_type=jnp.float32)
     part_back = jnp.einsum("vrd,vkd->vrk", arrive, weight_out, preferred_element_type=jnp.float32)
     pre_sum, back_sum = (
-        lax.psum(part_pre.astype(jnp.bfloat16), "tensor").astype(jnp.float32),
+        jnp.sum(lax.all_gather(part_pre.astype(jnp.bfloat16), "tensor"), axis=0).astype(
+            jnp.float32
+        ),
         lax.psum(part_back.astype(jnp.bfloat16), "tensor").astype(jnp.float32),
     )
     scaled = inv_rms[..., None]

time: 282 us -> 271 us (0.961)
  waiting for transfers between devices: 169 us -> 134 us
  matrix products: 61.7 us -> 72.8 us
  blocking collectives: 13.8 us -> 21 us
  other arithmetic: 12.9 us -> 18.7 us
    psum x3, waiting for transfers between devices: 37 us -> 12.3 us  [block_back(): lax.psum(part_back.astype(jnp.bfloat16), 'tensor').astype(jnp.float32)]
    dot_general x3, matrix products: 7.51 us -> 19.7 us  [block_back(): jnp.einsum('vrk,vrd->vkd', grad_scaled, gained, preferred_element_type=jn...]
    ppermute x2, waiting for transfers between devices: 38.8 us -> 28.4 us  [shifted(): return lax.ppermute(x, axis, [(i, (i + by) % count) for i in range(count)])]
    all_gather x0 -> x3, blocking collectives: none -> 7.12 us  [block_back(): lax.all_gather(part_pre.astype(jnp.bfloat16), 'tensor')]
    reduce_sum x0 -> x3, other arithmetic: none -> 3.47 us  [block_back(): jnp.sum(lax.all_gather(part_pre.astype(jnp.bfloat16), 'tensor'), axis=0)]
  transfers between devices with their start and end apart: 7 -> 7, of which waited for: 7 -> 6; matrix products, arithmetic and copies ran while one was open for 13% -> 24% of each run, Pallas kernels for 0% -> 0%
where the time goes in v1:
time: 271 us; the launch traced here: 270 us
  waiting for transfers between devices  134 us (49%)
  matrix products  72.8 us (27%)
  blocking collectives  21 us (8%)
  other arithmetic  18.7 us (7%)
  between operations  14.1 us (5%)
  starting transfers between devices  7.45 us (3%)
    reduce_scatter x1, waiting for transfers between devices, shards(): lax.psum_scatter((acc_in + add_in).astype(jnp.bfloat16), 'dp', scatter_di...  52.7 us
    reduce_scatter x1, waiting for transfers between devices, shards(): lax.psum_scatter((acc_out + add_out).astype(jnp.bfloat16), 'dp', scatter_...  41 us
    ppermute x2, waiting for transfers between devices, shifted(): return lax.ppermute(x, axis, [(i, (i + by) % count) for i in range(count)])  28.4 us
    dot_general x3, matrix products, block_back(): jnp.einsum('vrk,vrd->vkd', hidden, arrive, preferred_element_type=jnp.flo...  20.1 us
    dot_general x3, matrix products, block_back(): jnp.einsum('vrk,vrd->vkd', grad_scaled, gained, preferred_element_type=jn...  19.7 us
    dot_general x3, matrix products, block_back(): jnp.einsum('vrk,vkd->vrd', grad_scaled, weight_in, preferred_element_type...  14.7 us
    psum x3, waiting for transfers between devices, block_back(): lax.psum(part_back.astype(jnp.bfloat16), 'tensor').astype(jnp.float32)  12.3 us
    psum x1, blocking collectives, shards(): sums, counts = lax.psum((sums, counts), 'dp')  11.2 us
  transfers between devices with their start and end apart: 7, of which 6 were waited for; matrix products, arithmetic and copies ran while one was open for 24% of the time, Pallas kernels for 0%

profile of v1, /device:TPU:0, one launch (start us, length us, event | category | flops | bytes accessed | tf_op | source)
XLA Modules:
  0.0 270.4 jit_solution(16351129438634758896)
XLA Ops:
  7.3 4.9 %fusion.43 = bf16[2,128,512]{2,1,0:T(8,128)(2,1)} fusion(bf16[2,1,512,2048]{3,2,1,0:T(8,128)(2,1)} %param.11, bf16[2,1,128,2048]{3,2,1,0:T(8,128)(2,1)} %param.13), kind=kOutput, calls=%fused_computation.43 | convolution fusion | flops 537001984 | bytes 5505024 | tf_op jit(solution)/shard_map/vrd,vkd->vrk/dot_general | solution.py:24
  12.9 2.6 psum.42
  15.7 11.2 %all-reduce = (f32[4]{0:T(128)S(1)}, f32[4]{0:T(128)S(1)}) all-reduce(f32[4]{0:T(128)S(1)} %get-tuple-element.13, f32[4]{0:T(128)S(1)} %get-tuple-element.12), channel_id=1, replica_groups=mesh['pipe'=4,'dp'=4,'tensor'=2] {'dp'}, use_global_device_ids=true, to_apply=%region_8.9 | all-reduce | flops 8 | bytes 64 | tf_op jit(solution)/shard_map/psum | solution.py:74
  26.9 3.7 %fusion.52 = bf16[2,128,512]{2,1,0:T(8,128)(2,1)S(1)} fusion(bf16[2,1,512,2048]{3,2,1,0:T(8,128)(2,1)} %param.10, f32[2,2048]{1,0:T(2,128)S(1)} %bitcast.136, bf16[3,2,1,128,2048]{4,3,1,2,0:T(8,128)(2,1)S(1)} %bitcast.124), kind=kOutput, calls=%fused_computation.46 | convolution fusion | flops 538574848 | bytes 5521408 | tf_op jit(solution)/shard_map/vrd,vkd->vrk/dot_general | solution.py:23
  30.7 2.3 all-gather
  34.3 1.4 fusion.93
  35.7 4.9 %fusion.33 = bf16[2,128,2048]{2,1,0:T(8,128)(2,1)} fusion(bf16[2,1,512,2048]{3,2,1,0:T(8,128)(2,1)} %param.10, bf16[2,1,128,2048]{3,2,1,0:T(8,128)(2,1)} %param.13, f32[2,128]{1,0:T(2,128)S(1)} %fusion.121, f32[2,2048]{1,0:T(2,128)S(1)} %bitcast.137, bf16[3,2,1,128,2048]{4,3,1,2,0:T(8,128)(2,1)S(1)} %bitcast.125, f32[2,128]{1,0:T(2,128)S(1)} %get-tuple-element.22, ...), kind=kOutput, calls=%fused_computation.32 | convolution fusion | flops 542244864 | bytes 7882752 | tf_op jit(solution)/shard_map/vrk,vkd->vrd/dot_general | solution.py:38
  40.6 3.6 %collective-permute-start = (bf16[2,128,2048]{2,1,0:T(8,128)(2,1)}, bf16[2,128,2048]{2,1,0:T(8,128)(2,1)}, u32[]{:S(2)}, u32[]{:S(2)}) collective-permute-start(bf16[2,128,2048]{2,1,0:T(8,128)(2,1)} %fusion.33), channel_id=1, source_target_pairs={{0,24},{8,0},{16,8},{24,16},{1,25},{9,1},{17,9},{25,17},{2,26},{10... | collective-permute-start | bytes 3145736 | tf_op jit(solution)/shard_map/ppermute | solution.py:12
  44.5 1.6 multiply_convert_fusion
  46.2 21.0 %collective-permute-done = bf16[2,128,2048]{2,1,0:T(8,128)(2,1)} collective-permute-done((bf16[2,128,2048]{2,1,0:T(8,128)(2,1)}, bf16[2,128,2048]{2,1,0:T(8,128)(2,1)}, u32[]{:S(2)}, u32[]{:S(2)}) %collective-permute-start) | collective-permute-done | bytes 1048608 | tf_op jit(solution)/shard_map/ppermute | solution.py:12
  69.5 2.2 fusion.46
  71.8 3.7 %fusion.55 = bf16[2,128,512]{2,1,0:T(8,128)(2,1)S(1)} fusion(bf16[2,1,512,2048]{3,2,1,0:T(8,128)(2,1)} %param.10, f32[2,2048]{1,0:T(2,128)S(1)} %bitcast.138, bf16[3,2,1,128,2048]{4,3,1,2,0:T(8,128)(2,1)S(1)} %bitcast.126), kind=kOutput, calls=%fused_computation.47 | convolution fusion | flops 538574848 | bytes 5521408 | tf_op jit(solution)/shard_map/vrd,vkd->vrk/dot_general | solution.py:23
  75.5 2.3 all-gather.1
  79.0 12.1 %all-reduce.7.cloned.1.call-done = bf16[2,128,512]{2,1,0:T(8,128)(2,1)} async-done(((bf16[2,128,512]{2,1,0:T(8,128)(2,1)}), bf16[2,128,512]{2,1,0:T(8,128)(2,1)}) %all-reduce.7.cloned.1.call-update) | async-done | bytes 262160 | tf_op jit(solution)/shard_map/psum | solution.py:29
  92.5 5.0 %fusion.39 = bf16[2,128,2048]{2,1,0:T(8,128)(2,1)} fusion(f32[2,128]{1,0:T(2,128)S(1)} %fusion.123, bf16[2,1,512,2048]{3,2,1,0:T(8,128)(2,1)} %param.10, f32[2,2048]{1,0:T(2,128)S(1)} %bitcast.139, bf16[3,2,1,128,2048]{4,3,1,2,0:T(8,128)(2,1)S(1)} %bitcast.127, bf16[1,128,2048]{2,1,0:T(8,128)(2,1)} %copy-done.13, bf16[1,128,2048]{2,1,0:T(8,128)(2,1)} %copy-done.11, ...), kind=kOutput, calls=%fused_computation.36 | convolution fusion | flops 542769152 | bytes 7882752 | tf_op jit(solution)/shard_map/vrk,vkd->vrd/dot_general | solution.py:38
  97.4 3.6 %collective-permute-start.1 = (bf16[2,128,2048]{2,1,0:T(8,128)(2,1)}, bf16[2,128,2048]{2,1,0:T(8,128)(2,1)}, u32[]{:S(2)}, u32[]{:S(2)}) collective-permute-start(bf16[2,128,2048]{2,1,0:T(8,128)(2,1)} %fusion.39), channel_id=1, source_target_pairs={{0,24},{8,0},{16,8},{24,16},{1,25},{9,1},{17,9},{25,17},{2,26},{10... | collective-permute-start | bytes 3145736 | tf_op jit(solution)/shard_map/ppermute | solution.py:12
  101.1 1.5 fusion.58
  102.6 2.5 all-gather.2
  106.3 6.0 %fusion.62 = f32[2,512,2048]{2,1,0:T(8,128)} fusion(bf16[2,1,128,2048]{3,2,1,0:T(8,128)(2,1)} %param.13, bf16[2,128,512]{2,1,0:T(8,128)(2,1)} %copy-done.5, f32[2,128]{1,0:T(2,128)S(1)} %get-tuple-element.22), kind=kOutput, calls=%fused_computation.55 | convolution fusion | flops 537788416 | bytes 9700352 | tf_op jit(solution)/shard_map/vrk,vrd->vkd/dot_general | solution.py:37
  112.3 4.6 %fusion.110 = f32[2,512,2048]{2,1,0:T(8,128)} fusion(bf16[1,128,2048]{2,1,0:T(8,128)(2,1)S(1)} %copy-done.14, bf16[1,128,2048]{2,1,0:T(8,128)(2,1)S(1)} %copy-done.12, bf16[2,128,512]{2,1,0:T(8,128)(2,1)S(1)} %copy-done.7, f32[2,128]{1,0:T(2,128)S(1)} %get-tuple-element.21), kind=kOutput, calls=%fused_computation.106 | convolution fusion | flops 538312704 | bytes 9700352 | tf_op jit(solution)/shard_map/vrk,vrd->vkd/dot_general | solution.py:37
  116.9 7.3 %collective-permute-done.1 = bf16[2,128,2048]{2,1,0:T(8,128)(2,1)} collective-permute-done((bf16[2,128,2048]{2,1,0:T(8,128)(2,1)}, bf16[2,128,2048]{2,1,0:T(8,128)(2,1)}, u32[]{:S(2)}, u32[]{:S(2)}) %collective-permute-start.1) | collective-permute-done | bytes 1048608 | tf_op jit(solution)/shard_map/ppermute | solution.py:12
  126.5 2.2 fusion.49
  128.8 9.5 %add_convert_fusion = bf16[2,512,2048]{2,1,0:T(8,128)(2,1)} fusion(f32[2,512,2048]{2,1,0:T(8,128)} %fusion.62, f32[2,512,2048]{2,1,0:T(8,128)} %fusion.110, bf16[1,128,2048]{2,1,0:T(8,128)(2,1)} %copy-done.10, bf16[1,128,2048]{2,1,0:T(8,128)(2,1)} %copy-done.9, bf16[2,128,512]{2,1,0:T(8,128)(2,1)S(1)} %reduce_sum.130, f32[2,128]{1,0:T(2,128)S(1)} %get-tuple-element.20), kind=kOutput, calls=%fused_computation | convolution fusion | flops 544604160 | bytes 22283264 | tf_op jit(solution)/shard_map/vrk,vrd->vkd/dot_general | solution.py:37
  138.4 5.7 %fusion.74 = f32[2,512,2048]{2,1,0:T(8,128)} fusion(f32[2,2048]{1,0:T(2,128)S(1)} %bitcast.141, bf16[3,2,1,128,2048]{4,3,1,2,0:T(8,128)(2,1)S(1)} %bitcast.129, f32[2,128]{1,0:T(2,128)S(1)} %get-tuple-element.22, bf16[2,128,512]{2,1,0:T(8,128)(2,1)} %copy-done.5, bf16[2,128,512]{2,1,0:T(8,128)(2,1)} %all-reduce.5.cloned.1.call-done), kind=kOutput, calls=%fused_computation.59 | convolution fusion | flops 540147712 | bytes 9978880 | tf_op jit(solution)/shard_map/vrk,vrd->vkd/dot_general | solution.py:36
  144.1 4.6 %fusion.71 = f32[2,512,2048]{2,1,0:T(8,128)} fusion(f32[2,2048]{1,0:T(2,128)S(1)} %bitcast.142, bf16[3,2,1,128,2048]{4,3,1,2,0:T(8,128)(2,1)S(1)} %bitcast.130, f32[2,128]{1,0:T(2,128)S(1)} %get-tuple-element.21, bf16[2,128,512]{2,1,0:T(8,128)(2,1)S(1)} %copy-done.8, bf16[2,128,512]{2,1,0:T(8,128)(2,1)S(1)} %copy-done.15), kind=kOutput, calls=%fused_computation.58 | convolution fusion | flops 540147712 | bytes 9978880 | tf_op jit(solution)/shard_map/vrk,vrd->vkd/dot_general | solution.py:36
  149.0 9.4 %add_convert_fusion.1 = bf16[2,512,2048]{2,1,0:T(8,128)(2,1)} fusion(f32[2,512,2048]{2,1,0:T(8,128)} %fusion.74, f32[2,512,2048]{2,1,0:T(8,128)} %fusion.71, f32[2,2048]{1,0:T(2,128)S(1)} %bitcast.143, bf16[3,2,1,128,2048]{4,3,1,2,0:T(8,128)(2,1)S(1)} %bitcast.131, f32[2,128]{1,0:T(2,128)S(1)} %get-tuple-element.20, ...), kind=kOutput, calls=%fused_computation.1 | convolution fusion | flops 546439168 | bytes 22561792 | tf_op jit(solution)/shard_map/vrk,vrd->vkd/dot_general | solution.py:36
  158.4 1.4 fusion.109
  159.8 4.9 %fusion.61 = bf16[2,1,128,2048]{3,2,1,0:T(8,128)(2,1)} fusion(f32[2,128]{1,0:T(2,128)S(1)} %fusion.125, bf16[2,1,512,2048]{3,2,1,0:T(8,128)(2,1)} %param.10, f32[2,2048]{1,0:T(2,128)S(1)} %bitcast.144, bf16[3,2,1,128,2048]{4,3,1,2,0:T(8,128)(2,1)S(1)} %bitcast.132, bf16[1,128,2048]{2,1,0:T(8,128)(2,1)} %copy-done.10, bf16[1,128,2048]{2,1,0:T(8,128)(2,1)} %copy-done.9, ...), kind=kOutput, calls=%fused_computation.49 | convolution fusion | flops 542769152 | bytes 7882752 | tf_op jit(solution)/shard_map/vrk,vkd->vrd/dot_general | solution.py:38
  164.7 41.0 %reduce-scatter.5.cloned.1.call-done = bf16[2,128,2048]{2,1,0:T(8,128)(2,1)} async-done(((bf16[2,512,2048]{2,1,0:T(8,128)(2,1)}), bf16[2,128,2048]{2,1,0:T(8,128)(2,1)}) %reduce-scatter.5.cloned.1.call-update) | async-done | bytes 1048592 | tf_op jit(solution)/shard_map/reduce_scatter | solution.py:113
  205.7 2.8 %multiply_bitcast_fusion = f32[2,1,128,2048]{3,2,1,0:T(8,128)} fusion(bf16[2,128,2048]{2,1,0:T(8,128)(2,1)} %reduce-scatter.5.cloned.1.call-done), kind=kLoop, calls=%fused_computation.40 | loop fusion | flops 1048576 | bytes 3145728
  208.4 52.7 %reduce-scatter.3.cloned.1.call-done = bf16[2,128,2048]{2,1,0:T(8,128)(2,1)} async-done(((bf16[2,512,2048]{2,1,0:T(8,128)(2,1)}), bf16[2,128,2048]{2,1,0:T(8,128)(2,1)}) %reduce-scatter.3.cloned.1.call-update) | async-done | bytes 1048592 | tf_op jit(solution)/shard_map/reduce_scatter | solution.py:110
  261.1 2.8 %multiply_bitcast_fusion.1 = f32[2,1,128,2048]{3,2,1,0:T(8,128)} fusion(bf16[2,128,2048]{2,1,0:T(8,128)(2,1)} %reduce-scatter.3.cloned.1.call-done), kind=kLoop, calls=%fused_computation.41 | loop fusion | flops 1048576 | bytes 3145728
  (75 shorter events, 11.3 us)
Async XLA Ops:
  7.2 5.1 %copy-start.16 = (f32[2,1,2048]{2,1,0:T(1,128)S(1)}, f32[2,1,2048]{2,1,0:T(1,128)}, u32[]{:S(2)}) copy-start(f32[2,1,2048]{2,1,0:T(1,128)} %param.12) | copy-start | bytes 49156
  7.2 5.1 %copy-start = (bf16[3,2,1,128,2048]{4,3,2,1,0:T(8,128)(2,1)S(1)}, bf16[3,2,1,128,2048]{4,3,2,1,0:T(8,128)(2,1)}, u32[]{:S(2)}) copy-start(bf16[3,2,1,128,2048]{4,3,2,1,0:T(8,128)(2,1)} %param.9) | copy-start | bytes 9437188
  7.2 8.4 %copy-start.18 = (s32[2,1,4]{2,1,0:T(1,128)S(1)}, s32[2,1,4]{2,1,0:T(1,128)}, u32[]{:S(2)}) copy-start(s32[2,1,4]{2,1,0:T(1,128)} %param.17) | copy-start | bytes 100
  7.2 8.4 %copy-start.17 = (f32[2,1,4]{2,1,0:T(1,128)S(1)}, f32[2,1,4]{2,1,0:T(1,128)}, u32[]{:S(2)}) copy-start(f32[2,1,4]{2,1,0:T(1,128)} %param.15) | copy-start | bytes 100
  7.2 27.1 %all-reduce.5.cloned.1.call-start = ((), (), s32[]{:S(2)}) async-start(), calls=%async_computation.2 | async-start | bytes 524288 | tf_op jit(solution)/shard_map/psum | solution.py:29
  12.2 78.9 %all-reduce.7.cloned.1.call-start = ((), (), s32[]{:S(2)}) async-start(), calls=%async_computation.3 | async-start | bytes 524288 | tf_op jit(solution)/shard_map/psum | solution.py:29
  26.9 7.2 %copy-start.19 = (s32[2,1,4]{2,1,0:T(1,128)S(1)}, s32[2,1,4]{2,1,0:T(1,128)}, u32[]{:S(2)}) copy-start(s32[2,1,4]{2,1,0:T(1,128)} %param.16) | copy-start | bytes 100
  34.1 6.5 %copy-start.5 = (bf16[2,128,512]{2,1,0:T(8,128)(2,1)}, bf16[2,128,512]{2,1,0:T(8,128)(2,1)S(1)}, u32[]{:S(2)}) copy-start(bf16[2,128,512]{2,1,0:T(8,128)(2,1)S(1)} %reduce_sum.120) | copy-start | bytes 786436
  40.6 26.6 %collective-permute-start = (bf16[2,128,2048]{2,1,0:T(8,128)(2,1)}, bf16[2,128,2048]{2,1,0:T(8,128)(2,1)}, u32[]{:S(2)}, u32[]{:S(2)}) collective-permute-start(bf16[2,128,2048]{2,1,0:T(8,128)(2,1)} %fusion.33), channel_id=1, source_target_pairs={{0,24},{8,0},{16,8},{24,16},{1,25},{9,1},{17,9},{25,17},{2,26},{10... | collective-permute-start | bytes 3145736 | tf_op jit(solution)/shard_map/ppermute | solution.py:12
  44.5 24.9 %copy-start.1 = (bf16[2,1,512,2048]{3,2,1,0:T(8,128)(2,1)S(1)}, bf16[2,1,512,2048]{3,2,1,0:T(8,128)(2,1)}, u32[]{:S(2)}) copy-start(bf16[2,1,512,2048]{3,2,1,0:T(8,128)(2,1)} %param.11) | copy-start | bytes 12582916
  46.1 21.1 %copy-start.3 = (bf16[2,128,2048]{2,1,0:T(8,128)(2,1)}, bf16[2,128,2048]{2,1,0:T(8,128)(2,1)S(1)}, u32[]{:S(2)}) copy-start(bf16[2,128,2048]{2,1,0:T(8,128)(2,1)S(1)} %multiply_convert_fusion) | copy-start | bytes 3145732
  68.5 0.8 copy-start.11
  68.5 1.0 copy-start.13
  71.7 77.3 %all-reduce.9.cloned.1.call-start = ((), (), s32[]{:S(2)}) async-start(), calls=%async_computation.4 | async-start | bytes 524288 | tf_op jit(solution)/shard_map/psum | solution.py:29
  79.0 18.5 %copy-start.6 = (bf16[2,128,512]{2,1,0:T(8,128)(2,1)}, bf16[2,128,512]{2,1,0:T(8,128)(2,1)S(1)}, u32[]{:S(2)}) copy-start(bf16[2,128,512]{2,1,0:T(8,128)(2,1)S(1)} %reduce_sum.128) | copy-start | bytes 786436
  92.4 8.6 %copy-start.20 = (bf16[2,1,512,2048]{3,2,1,0:T(8,128)(2,1)S(1)}, bf16[2,1,512,2048]{3,2,1,0:T(8,128)(2,1)}, u32[]{:S(2)}) copy-start(bf16[2,1,512,2048]{3,2,1,0:T(8,128)(2,1)} %param.10) | copy-start | bytes 12582916
  97.4 26.8 %collective-permute-start.1 = (bf16[2,128,2048]{2,1,0:T(8,128)(2,1)}, bf16[2,128,2048]{2,1,0:T(8,128)(2,1)}, u32[]{:S(2)}, u32[]{:S(2)}) collective-permute-start(bf16[2,128,2048]{2,1,0:T(8,128)(2,1)} %fusion.39), channel_id=1, source_target_pairs={{0,24},{8,0},{16,8},{24,16},{1,25},{9,1},{17,9},{25,17},{2,26},{10... | collective-permute-start | bytes 3145736 | tf_op jit(solution)/shard_map/ppermute | solution.py:12
  106.2 6.0 %copy-start.7 = (bf16[2,128,512]{2,1,0:T(8,128)(2,1)S(1)}, bf16[2,128,512]{2,1,0:T(8,128)(2,1)}, u32[]{:S(2)}) copy-start(bf16[2,128,512]{2,1,0:T(8,128)(2,1)} %copy-done.6) | copy-start | bytes 786436
  106.2 6.0 %copy-start.12 = (bf16[1,128,2048]{2,1,0:T(8,128)(2,1)S(1)}, bf16[1,128,2048]{2,1,0:T(8,128)(2,1)}, u32[]{:S(2)}) copy-start(bf16[1,128,2048]{2,1,0:T(8,128)(2,1)} %copy-done.11) | copy-start | bytes 1572868
  106.3 6.0 %copy-start.14 = (bf16[1,128,2048]{2,1,0:T(8,128)(2,1)S(1)}, bf16[1,128,2048]{2,1,0:T(8,128)(2,1)}, u32[]{:S(2)}) copy-start(bf16[1,128,2048]{2,1,0:T(8,128)(2,1)} %copy-done.13) | copy-start | bytes 1572868
  112.3 11.9 %copy-start.4 = (bf16[2,128,2048]{2,1,0:T(8,128)(2,1)S(1)}, bf16[2,128,2048]{2,1,0:T(8,128)(2,1)}, u32[]{:S(2)}) copy-start(bf16[2,128,2048]{2,1,0:T(8,128)(2,1)} %copy-done.3) | copy-start | bytes 3145732
  112.3 14.2 %copy-start.2 = (bf16[2,1,512,2048]{3,2,1,0:T(8,128)(2,1)S(1)}, bf16[2,1,512,2048]{3,2,1,0:T(8,128)(2,1)}, u32[]{:S(2)}) copy-start(bf16[2,1,512,2048]{3,2,1,0:T(8,128)(2,1)} %param.11) | copy-start | bytes 12582916
  125.5 0.8 copy-start.9
  125.6 1.0 copy-start.10
  128.8 76.9 %reduce-scatter.5.cloned.1.call-start = ((), (), s32[]{:S(2)}) async-start(), calls=%async_computation.6 | async-start | bytes 5242880 | tf_op jit(solution)/shard_map/reduce_scatter | solution.py:113
  138.3 122.8 %reduce-scatter.3.cloned.1.call-start = ((), (), s32[]{:S(2)}) async-start(), calls=%async_computation.5 | async-start | bytes 5242880 | tf_op jit(solution)/shard_map/reduce_scatter | solution.py:110
  138.3 5.8 %copy-start.8 = (bf16[2,128,512]{2,1,0:T(8,128)(2,1)S(1)}, bf16[2,128,512]{2,1,0:T(8,128)(2,1)}, u32[]{:S(2)}) copy-start(bf16[2,128,512]{2,1,0:T(8,128)(2,1)} %copy-done.6) | copy-start | bytes 786436
  138.3 5.7 %copy-start.15 = (bf16[2,128,512]{2,1,0:T(8,128)(2,1)S(1)}, bf16[2,128,512]{2,1,0:T(8,128)(2,1)}, u32[]{:S(2)}) copy-start(bf16[2,128,512]{2,1,0:T(8,128)(2,1)} %all-reduce.7.cloned.1.call-done) | copy-start | bytes 786436
Sparse Core Ops, SparseCore 0:
  12.3 20.9 all-reduce.4
  71.8 19.1 all-reduce.6
  128.9 20.0 all-reduce.8
  151.8 53.7 reduce-scatter.4
  208.5 52.5 reduce-scatter.2
